TPU v7x, 32 devices: a whole 2x2x4 slice. The times are simulated.
32 devices in a mesh: unit: 2 (over core), zero: 4 (over z), model: 4 (over y, x).
Axes of the slice: x: 2, y: 2, z: 4, core: 2. Of those that a mesh axis runs over, the one named last changes fastest.
Arguments:
- first_query: float32 [16384, 8192], P(('unit', 'zero'), 'model'), parts along dimension 0, may hold values from -0.09375 to 0.09375
- second_query: float32 [16384, 8192], P(('unit', 'zero'), 'model'), parts along dimension 0, may hold values from -0.0625 to 0.0625
- first_key: float32 [16384, 1024], P(('unit', 'zero'), 'model'), parts along dimension 0, may hold values from -0.09375 to 0.09375
- second_key: float32 [16384, 1024], P(('unit', 'zero'), 'model'), parts along dimension 0, may hold values from -0.0625 to 0.0625
- first_value: float32 [16384, 1024], P(('unit', 'zero'), 'model'), parts along dimension 0, may hold values from -0.09375 to 0.09375
- second_value: float32 [16384, 1024], P(('unit', 'zero'), 'model'), parts along dimension 0, may hold values from -0.0625 to 0.0625
- mix_share: float32 [16384], P(('unit', 'zero')), parts along dimension 0, may hold values from 0.2 to 0.8
- norm_train: float32 [16384], P(('unit', 'zero', 'model')), parts along dimension 0, may hold values from 0.25 to 1.75
- norm_step: float32 [16384], P(('unit', 'zero', 'model')), parts along dimension 0, may hold values from -0.3 to 0.3
Outputs:
- serve_query: bfloat16 [16384, 8192], P('unit', 'model'), parts along dimension 0
- serve_key: bfloat16 [16384, 1024], P('unit', 'model'), parts along dimension 0
- serve_value: bfloat16 [16384, 1024], P('unit', 'model'), parts along dimension 0
- factor_query: float32 [16384], P(('unit', 'model')), parts along dimension 0
- factor_key: float32 [2048], P(('unit', 'model')), parts along dimension 0
- factor_value: float32 [2048], P(('unit', 'model')), parts along dimension 0
- serve_norm: bfloat16 [16384], P('unit'), parts along dimension 0
There are 2 independent parts, one for each index of `unit`. A program takes and returns all parts, laid end to end along the dimension named above; each array names one. Nothing has to cross between parts.
All inputs are finite; a program needn't handle non-finite values.
Results may differ from a plain program's by a relative error of at most 0.0004.
Values may be sent and summed in bfloat16 or wider, within the bound.
No kernel may reach another device: no remote copies, remote signals or barrier semaphores. Data moves between devices by JAX's collectives and lax.ppermute only.
A program may use at most 192 MiB of HBM per device.

v0:
```python
import jax
import jax.numpy as jnp
from jax import lax
from jax.sharding import PartitionSpec as P


def on_device(
    first_query,
    second_query,
    first_key,
    second_key,
    first_value,
    second_value,
    mix_share,
    norm_train,
    norm_step,
):
    fresh_query = mix_share[:, None] * first_query + (1.0 - mix_share[:, None]) * second_query
    fresh_key = mix_share[:, None] * first_key + (1.0 - mix_share[:, None]) * second_key
    fresh_value = mix_share[:, None] * first_value + (1.0 - mix_share[:, None]) * second_value
    total_query, total_key, total_value = lax.psum(
        (
            jnp.sum(fresh_query * fresh_query, axis=0),
            jnp.sum(fresh_key * fresh_key, axis=0),
            jnp.sum(fresh_value * fresh_value, axis=0),
        ),
        "zero",
    )
    factor_query = jnp.sqrt(total_query)
    factor_key = jnp.sqrt(total_key)
    factor_value = jnp.sqrt(total_value)
    narrow_query, narrow_key, narrow_value = (
        (fresh_query / factor_query).astype(jnp.bfloat16),
        (fresh_key / factor_key).astype(jnp.bfloat16),
        (fresh_value / factor_value).astype(jnp.bfloat16),
    )
    serve_query, serve_key, serve_value = (
        lax.all_gather(narrow_query, "zero", axis=0, tiled=True),
        lax.all_gather(narrow_key, "zero", axis=0, tiled=True),
        lax.all_gather(narrow_value, "zero", axis=0, tiled=True),
    )
    serve_norm = lax.all_gather(
        (norm_train + norm_step).astype(jnp.bfloat16), ("zero", "model"), axis=0, tiled=True
    )
    return (serve_query, serve_key, serve_value, factor_query, factor_key, factor_value, serve_norm)


def solution(mesh):
    in_specs = (
        P(("unit", "zero"), "model"),
        P(("unit", "zero"), "model"),
        P(("unit", "zero"), "model"),
        P(("unit", "zero"), "model"),
        P(("unit", "zero"), "model"),
        P(("unit", "zero"), "model"),
        P(("unit", "zero")),
        P(("unit", "zero", "model")),
        P(("unit", "zero", "model")),
    )
    out_specs = (
        P("unit", "model"),
        P("unit", "model"),
        P("unit", "model"),
        P(("unit", "model")),
        P(("unit", "model")),
        P(("unit", "model")),
        P("unit"),
    )
    return jax.shard_map(
        on_device, mesh=mesh, in_specs=in_specs, out_specs=out_specs, check_vma=False
    )
```

profile of v0, /device:TPU:0, one launch (start us, length us, event | category | flops | bytes accessed | tf_op | source)
XLA Modules:
  0.0 805.4 jit_solution(15348338283091460513)
XLA Ops:
  7.2 0.0 all-gather.7.cloned.1.call-start
  7.2 0.7 broadcast_subtract_fusion
  7.9 0.0 copy-start
  7.9 0.0 copy-start.1
  7.9 0.0 copy-start.2
  7.9 0.0 copy-start.3
  7.9 0.0 copy-start.5
  7.9 12.1 %multiply_reduce_fusion = f32[2048]{0:T(1024)S(1)} fusion(f32[2048,2048]{1,0:T(8,128)} %param.10, f32[2048]{0:T(1024)S(1)} %broadcast_subtract_fusion, f32[2048,2048]{1,0:T(8,128)} %param.9, f32[2048]{0:T(1024)} %param.15), kind=kLoop, calls=%fused_computation.1 | loop fusion | flops 20969472 | bytes 33579008 | tf_op jit(solution)/shard_map/reduce_sum | solution.py:23
  20.1 0.0 copy-done
  20.1 0.0 copy-done.1
  20.1 0.3 copy-done.2
  20.4 0.6 copy-done.3
  21.0 0.0 copy-done.5
  21.0 0.9 multiply_reduce_fusion.1
  21.9 20.4 %all-reduce = (f32[2048]{0:T(1024)S(1)}, f32[256]{0:T(256)S(1)}, f32[256]{0:T(256)S(1)}) all-reduce(f32[2048]{0:T(1024)S(1)} %multiply_reduce_fusion, f32[256]{0:T(256)S(1)} %get-tuple-element.8, f32[256]{0:T(256)S(1)} %get-tuple-element.7), channel_id=1, replica_groups=mesh['unit'=2,'zero'=4,'model'=4] {'zero'}, use_global_device_ids=true, to_apply=%region_1.0 | all-reduce | flops 2560 | bytes 20480 | tf_op jit(solution)/shard_map/psum | solution.py:21
  42.3 0.0 copy-start.7
  42.3 0.0 copy-start.8
  42.3 4.2 divide_convert_fusion.1
  46.5 0.0 copy-done.7
  46.5 0.0 copy-done.8
  46.5 0.0 all-gather.7.cloned.1.call-update
  46.6 0.0 all-gather.9.cloned.1.call-start
  46.6 0.7 all-gather.9.cloned.1.call-update
  47.3 0.0 all-gather.5.cloned.1.call-start
  47.4 0.0 copy-start.6
  47.4 16.0 %divide_convert_fusion = bf16[2048,2048]{1,0:T(8,128)(2,1)} fusion(f32[2048]{0:T(1024)S(1)} %sqrt.9, f32[2048,2048]{1,0:T(8,128)} %param.10, f32[2048]{0:T(1024)S(1)} %broadcast_subtract_fusion, f32[2048,2048]{1,0:T(8,128)} %param.9, f32[2048]{0:T(1024)S(1)} %copy-done.5), kind=kLoop, calls=%fused_computation | loop fusion | flops 20971520 | bytes 41967616 | tf_op jit(solution)/shard_map/convert_element_type | solution.py:33
  63.4 0.0 copy-done.6
  63.4 0.0 copy-start.9
  63.4 0.0 copy-start.10
  63.4 0.0 all-gather.5.cloned.1.call-update
  63.4 0.6 copy-done.9
  64.1 0.0 copy-done.10
  64.1 38.9 %all-gather = bf16[16,1,512]{2,1,0:T(2,128)(2,1)S(1)} all-gather(bf16[1,1,512]{2,1,0:T(2,128)(2,1)S(1)} %reshape.20), channel_id=1, replica_groups=mesh['unit'=2,'zero'=4,'model'=4] {'zero','model'}, dimensions={0}, use_global_device_ids=true | all-gather | bytes 17408 | tf_op jit(solution)/shard_map/all_gather | solution.py:42
  103.0 0.1 reduce
  103.1 0.6 copy.16
  103.7 22.2 %all-gather.7.cloned.1.call-done = bf16[8192,256]{1,0:T(8,128)(2,1)} async-done(((bf16[2048,256]{1,0:T(8,128)(2,1)}), bf16[8192,256]{1,0:T(8,128)(2,1)}) %all-gather.7.cloned.1.call-update) | async-done | bytes 4194320 | tf_op jit(solution)/shard_map/all_gather | solution.py:39
  126.0 81.3 %all-gather.9.cloned.1.call-done = bf16[8192,256]{1,0:T(8,128)(2,1)} async-done(((bf16[2048,256]{1,0:T(8,128)(2,1)}), bf16[8192,256]{1,0:T(8,128)(2,1)}) %all-gather.9.cloned.1.call-update) | async-done | bytes 4194320 | tf_op jit(solution)/shard_map/all_gather | solution.py:40
  207.3 562.0 %all-gather.5.cloned.1.call-done = bf16[8192,2048]{1,0:T(8,128)(2,1)} async-done(((bf16[2048,2048]{1,0:T(8,128)(2,1)}), bf16[8192,2048]{1,0:T(8,128)(2,1)}) %all-gather.5.cloned.1.call-update) | async-done | bytes 33554448 | tf_op jit(solution)/shard_map/all_gather | solution.py:38
  769.3 22.9 %copy.20 = bf16[8192,2048]{1,0:T(8,128)(2,1)} copy(bf16[8192,2048]{1,0:T(8,128)(2,1)} %all-gather.5.cloned.1.call-done) | data formatting | bytes 67108864
  792.2 0.0 copy-start.4
  792.2 4.6 copy.21
  796.8 0.0 copy-done.4
  796.8 2.0 copy.22
  (5 shorter events, 0.0 us)
Async XLA Ops:
  7.2 118.8 %all-gather.7.cloned.1.call-start = ((), (), s32[]{:S(2)}) async-start(), calls=%async_computation.1 | async-start | bytes 5242880 | tf_op jit(solution)/shard_map/all_gather | solution.py:39
  7.9 12.2 %copy-start = (f32[2048,256]{1,0:T(8,128)S(1)}, f32[2048,256]{1,0:T(8,128)}, u32[]{:S(2)}) copy-start(f32[2048,256]{1,0:T(8,128)} %param.14) | copy-start | bytes 6291460
  7.9 12.2 %copy-start.1 = (f32[2048,256]{1,0:T(8,128)S(1)}, f32[2048,256]{1,0:T(8,128)}, u32[]{:S(2)}) copy-start(f32[2048,256]{1,0:T(8,128)} %param.13) | copy-start | bytes 6291460
  7.9 12.5 %copy-start.2 = (f32[2048,256]{1,0:T(8,128)S(1)}, f32[2048,256]{1,0:T(8,128)}, u32[]{:S(2)}) copy-start(f32[2048,256]{1,0:T(8,128)} %param.12) | copy-start | bytes 6291460
  7.9 13.1 %copy-start.3 = (f32[2048,256]{1,0:T(8,128)S(1)}, f32[2048,256]{1,0:T(8,128)}, u32[]{:S(2)}) copy-start(f32[2048,256]{1,0:T(8,128)} %param.11) | copy-start | bytes 6291460
  7.9 13.1 %copy-start.5 = (f32[2048]{0:T(1024)S(1)}, f32[2048]{0:T(1024)}, u32[]{:S(2)}) copy-start(f32[2048]{0:T(1024)} %param.15) | copy-start | bytes 24580
  42.3 4.2 copy-start.7
  42.3 4.2 copy-start.8
  46.6 160.7 %all-gather.9.cloned.1.call-start = ((), (), s32[]{:S(2)}) async-start(), calls=%async_computation.2 | async-start | bytes 5242880 | tf_op jit(solution)/shard_map/all_gather | solution.py:40
  47.3 722.0 %all-gather.5.cloned.1.call-start = ((), (), s32[]{:S(2)}) async-start(), calls=%async_computation | async-start | bytes 41943040 | tf_op jit(solution)/shard_map/all_gather | solution.py:38
  47.4 16.0 %copy-start.6 = (f32[2048]{0:T(1024)}, f32[2048]{0:T(1024)S(1)}, u32[]{:S(2)}) copy-start(f32[2048]{0:T(1024)S(1)} %sqrt.9) | copy-start | bytes 24580
  63.4 0.7 copy-start.9
  63.4 0.7 copy-start.10
  792.2 4.6 copy-start.4
Sparse Core Ops, SparseCore 0:
  46.7 79.2 all-gather.6
  128.1 79.1 all-gather.8
  209.4 559.8 all-gather.4
where the time goes:
time: 806 us; the launch traced here: 805 us
  waiting for transfers between devices  666 us (83%)
  blocking collectives  59.3 us (7%)
  other arithmetic  34 us (4%)
  local copies, waits for them, and re-layouts  31.8 us (4%)
  between operations  13.8 us (2%)
    all_gather x1, waiting for transfers between devices, on_device(): lax.all_gather(narrow_query, 'zero', axis=0, tiled=True)  562 us
    all_gather x1, waiting for transfers between devices, on_device(): lax.all_gather(narrow_value, 'zero', axis=0, tiled=True)  81.3 us
    all_gather x1, blocking collectives, on_device(): lax.all_gather((norm_train + norm_step).astype(jnp.bfloat16), ('zero', 'm...  38.9 us
    unnamed x27, local copies, waits for them, and re-layouts  31.8 us
    all_gather x1, waiting for transfers between devices, on_device(): lax.all_gather(narrow_key, 'zero', axis=0, tiled=True)  22.2 us
    psum x1, blocking collectives, on_device(): lax.psum((jnp.sum(fresh_query * fresh_query, axis=0), jnp.sum(fresh_key *...  20.4 us
  transfers between devices with their start and end apart: 3, of which 3 were waited for; matrix products, arithmetic and copies ran while one was open for 2% of the time, Pallas kernels for 0%

commit v1 on v0

v1 whole, which is shorter than its diff:
```python
import functools

import jax
import jax.numpy as jnp
from jax import lax
from jax.experimental import pallas as pl
from jax.experimental.pallas import tpu as pltpu
from jax.sharding import PartitionSpec as P


PIECES = 8


def place_kernel(n, step, row, *refs):
    count = 3 if step == 1 else 2
    sources = refs[:count]
    out, buf, sem_in, sem_out = refs[count + 1 :]
    z = lax.axis_index("zero")
    rows = sources[0].shape[0]
    shard = out.shape[0] // n
    shards = [z + step, z - step, z]
    valid = [z + step < n, z >= step, None]

    def guarded(i, f):
        if valid[i] is None:
            f()
        else:
            pl.when(valid[i])(f)

    def take(i):
        return pltpu.make_async_copy(sources[i], buf.at[i], sem_in.at[i])

    def give(i):
        return pltpu.make_async_copy(
            buf.at[i], out.at[pl.ds(shards[i] * shard + row, rows)], sem_out.at[i]
        )

    for i in range(count):
        guarded(i, lambda i=i: take(i).start())
    for i in range(count):

        def pass_on(i=i):
            take(i).wait()
            give(i).start()

        guarded(i, pass_on)
    for i in range(count):
        guarded(i, lambda i=i: give(i).wait())


def place(n, step, row, out, *sources):
    rows, columns = sources[0].shape
    count = len(sources)
    any_spec = pl.BlockSpec(memory_space=pl.ANY)
    return pl.pallas_call(
        functools.partial(place_kernel, n, step, row),
        out_shape=jax.ShapeDtypeStruct(out.shape, out.dtype),
        in_specs=[any_spec] * (count + 1),
        out_specs=any_spec,
        input_output_aliases={count: 0},
        scratch_shapes=[
            pltpu.VMEM((count, rows, columns), out.dtype),
            pltpu.SemaphoreType.DMA((count,)),
            pltpu.SemaphoreType.DMA((count,)),
        ],
    )(*sources, out)


def blank_kernel(out):
    pass


def blank(shape, dtype):
    return pl.pallas_call(
        blank_kernel,
        out_shape=jax.ShapeDtypeStruct(shape, dtype),
        out_specs=pl.BlockSpec(memory_space=pl.ANY),
        name="blank",
    )()


def exchanged_sum(mine, n):
    if n > 4:
        return lax.psum(mine, "zero")
    z = lax.axis_index("zero")
    got = [mine]
    for k in range(1, n):
        got.append(lax.ppermute(mine, "zero", [(i, (i + k) % n) for i in range(n)]))
    ordered = [
        lax.select_n(lax.rem(z - i + n, n), *got) if n > 1 else mine for i in range(n)
    ]
    return sum(ordered[1:], ordered[0])


def on_device(
    n,
    first_query,
    second_query,
    first_key,
    second_key,
    first_value,
    second_value,
    mix_share,
    norm_train,
    norm_step,
):
    z = lax.axis_index("zero")
    share = mix_share[:, None]

    def squares(first, second):
        fresh = share * first + (1.0 - share) * second
        return jnp.sum(fresh * fresh, axis=0)

    def narrow(first, second, factor, row, rows):
        part = share[row : row + rows]
        fresh = part * first[row : row + rows] + (1.0 - part) * second[row : row + rows]
        return (fresh / factor).astype(jnp.bfloat16)

    wide = first_key.shape[1]
    rows = first_key.shape[0]
    mine_kv = jnp.concatenate((squares(first_key, second_key), squares(first_value, second_value)))
    factor_kv = jnp.sqrt(exchanged_sum(mine_kv, n))
    factor_key, factor_value = factor_kv[:wide], factor_kv[wide:]
    key = narrow(first_key, second_key, factor_key, 0, rows)
    first_value, second_value, key = lax.optimization_barrier((first_value, second_value, key))
    value = narrow(first_value, second_value, factor_value, 0, rows)

    mine_query = squares(first_query, second_query)
    factor_query = jnp.sqrt(exchanged_sum(mine_query, n))
    size = rows // PIECES
    queries = []
    for i in range(PIECES):
        queries.append(narrow(first_query, second_query, factor_query, i * size, size))
    norm = lax.all_gather((norm_train + norm_step).astype(jnp.bfloat16), "model", tiled=True)

    outs = [
        blank((n * rows, wide), jnp.bfloat16),
        blank((n * rows, wide), jnp.bfloat16),
        blank((n * rows, first_query.shape[1]), jnp.bfloat16),
    ]
    pieces = [(0, 0, key), (1, 0, value)] + [(2, i * size, q) for i, q in enumerate(queries)]
    lefts = [p for _, _, p in pieces]
    rights = [p for _, _, p in pieces]
    for j, step in sequence(n):
        which, row, own = pieces[j]
        lefts[j] = lax.ppermute(
            lefts[j], "zero", [(i, i - 1) for i in range(1, n - step + 1)]
        )
        rights[j] = lax.ppermute(rights[j], "zero", [(i, i + 1) for i in range(step - 1, n - 1)])
        sources = (lefts[j], rights[j]) + ((own,) if step == 1 else ())
        outs[which] = place(n, step, row, outs[which], *sources)
    full = jnp.zeros((n, norm.shape[0]), norm.dtype)
    full = lax.dynamic_update_index_in_dim(full, norm, z, 0)
    left = right = norm
    for step in range(1, n):
        left = lax.ppermute(left, "zero", [(i, i - 1) for i in range(1, n - step + 1)])
        right = lax.ppermute(right, "zero", [(i, i + 1) for i in range(step - 1, n - 1)])
        index = jnp.arange(n)[:, None]
        full = jnp.where(index == z + step, left[None], full)
        full = jnp.where(index == z - step, right[None], full)
    serve_norm = full.reshape(-1)
    return (outs[2], outs[0], outs[1], factor_query, factor_key, factor_value, serve_norm)


def sequence(n):
    query = range(2, 2 + PIECES)
    order = [(0, 1), (1, 1)]
    for step in range(1, n):
        if step + 1 < n:
            order += [(0, step + 1), (1, step + 1)]
        order += [(j, step) for j in query]
    return order


def solution(mesh):
    in_specs = (
        P(("unit", "zero"), "model"),
        P(("unit", "zero"), "model"),
        P(("unit", "zero"), "model"),
        P(("unit", "zero"), "model"),
        P(("unit", "zero"), "model"),
        P(("unit", "zero"), "model"),
        P(("unit", "zero")),
        P(("unit", "zero", "model")),
        P(("unit", "zero", "model")),
    )
    out_specs = (
        P("unit", "model"),
        P("unit", "model"),
        P("unit", "model"),
        P(("unit", "model")),
        P(("unit", "model")),
        P(("unit", "model")),
        P("unit"),
    )
    n = mesh.shape["zero"]

    def body(*args):
        return on_device(n, *args)

    return jax.shard_map(
        body, mesh=mesh, in_specs=in_specs, out_specs=out_specs, check_vma=False
    )
```

time: 806 us -> 761 us (0.944)
  waiting for transfers between devices: 666 us -> 534 us
  starting transfers between devices: 0.12 us -> 111 us
  Pallas kernels: 0 us -> 70.9 us
  blocking collectives: 59.3 us -> 8.1 us
  local copies, waits for them, and re-layouts: 31.8 us -> 2.52 us
  between operations: 13.8 us -> 2.5 us
    all_gather x3 -> x0, waiting for transfers between devices: 666 us -> none  [the longest x1 562 us: on_device(): lax.all_gather(narrow_query, 'zero', axis=0, tiled=True)]
    ppermute x0 -> x72, waiting for transfers between devices: none -> 534 us  [the longest x30 460 us: on_device(): lax.ppermute(lefts[j], 'zero', [(i, i - 1) for i in range(1, n - step + 1)])]
    ppermute x0 -> x72, starting transfers between devices: none -> 111 us  [the longest x30 53.4 us: on_device(): lax.ppermute(rights[j], 'zero', [(i, i + 1) for i in range(step - 1, n -...]
    pallas_call x0 -> x33, Pallas kernels: none -> 70.9 us  [the longest x30 70.9 us: place(): pl.pallas_call(functools.partial(place_kernel, n, step, row), out_shape=j...]
    all_gather x1, blocking collectives: 38.9 us -> 8.1 us  [on_device(): lax.all_gather((norm_train + norm_step).astype(jnp.bfloat16), 'model', ti...]
    unnamed x27 -> x145, local copies, waits for them, and re-layouts: 31.8 us -> 2.42 us
    psum x1 -> x0, blocking collectives: 20.4 us -> none  [on_device(): lax.psum((jnp.sum(fresh_query * fresh_query, axis=0), jnp.sum(fresh_key *...]
    convert_element_type x2 -> x4, other arithmetic: 20.2 us -> 15.7 us  [narrow(): return (fresh / factor).astype(jnp.bfloat16)]
  transfers between devices with their start and end apart: 3 -> 72, of which waited for: 3 -> 34; matrix products, arithmetic and copies ran while one was open for 2% -> 2% of each run, Pallas kernels for 0% -> 9%
where the time goes in v1:
time: 761 us; the launch traced here: 758 us
  waiting for transfers between devices  534 us (70%)
  starting transfers between devices  111 us (15%)
  Pallas kernels  70.9 us (9%)
  other arithmetic  29.6 us (4%)
  blocking collectives  8.1 us (1%)
    ppermute x30, waiting for transfers between devices, on_device(): lax.ppermute(lefts[j], 'zero', [(i, i - 1) for i in range(1, n - step + 1)])  460 us
    pallas_call x30, Pallas kernels, place(): pl.pallas_call(functools.partial(place_kernel, n, step, row), out_shape=j...  70.9 us
    ppermute x30, starting transfers between devices, on_device(): lax.ppermute(rights[j], 'zero', [(i, i + 1) for i in range(step - 1, n -...  53.4 us
    ppermute x30, waiting for transfers between devices, on_device(): lax.ppermute(rights[j], 'zero', [(i, i + 1) for i in range(step - 1, n -...  47 us
    ppermute x30, starting transfers between devices, on_device(): lax.ppermute(lefts[j], 'zero', [(i, i - 1) for i in range(1, n - step + 1)])  38.6 us
    ppermute x3, waiting for transfers between devices, on_device(): lax.ppermute(left, 'zero', [(i, i - 1) for i in range(1, n - step + 1)])  26.3 us
    convert_element_type x4, other arithmetic, narrow(): return (fresh / factor).astype(jnp.bfloat16)  15.7 us
  transfers between devices with their start and end apart: 72, of which 34 were waited for; matrix products, arithmetic and copies ran while one was open for 2% of the time, Pallas kernels for 9%

profile of v1, /device:TPU:0, one launch (start us, length us, event | category | flops | bytes accessed | tf_op | source)
XLA Modules:
  0.0 758.1 jit_solution(9728547555805053524)
XLA Ops:
  1.4 12.1 %multiply_reduce_fusion = f32[2048]{0:T(1024)S(1)} fusion(f32[2048,2048]{1,0:T(8,128)} %param.10, f32[2048,2048]{1,0:T(8,128)} %param.9, f32[2048]{0:T(1024)S(1)} %broadcast_subtract_fusion, f32[2048]{0:T(1024)} %param.15), kind=kLoop, calls=%fused_computation | loop fusion | flops 20969472 | bytes 33579008 | tf_op jit(solution)/shard_map/reduce_sum | solution.py:112
  13.5 3.1 collective-permute-start
  16.6 2.6 collective-permute-start.1
  24.1 8.1 %all-gather = bf16[4,1,512]{2,1,0:T(2,128)(2,1)S(1)} all-gather(bf16[1,1,512]{2,1,0:T(2,128)(2,1)S(1)} %reshape.92), channel_id=1, replica_groups=mesh['unit'=2,'zero'=4,'model'=4] {'model'}, dimensions={0}, use_global_device_ids=true | all-gather | bytes 5120 | tf_op jit(solution)/shard_map/all_gather | solution.py:134
  33.1 3.1 collective-permute-start.66
  43.1 2.7 divide_convert_fusion.refs_2_
  47.1 6.4 collective-permute-start.63
  56.9 6.7 divide_convert_fusion.2
  63.6 4.9 collective-permute-start.57
  68.5 24.9 %collective-permute-done.71 = bf16[2048]{0:T(1024)(128)(2,1)S(1)} collective-permute-done((bf16[2048]{0:T(1024)(128)(2,1)S(1)}, bf16[2048]{0:T(1024)(128)(2,1)S(1)}, u32[]{:S(2)}, u32[]{:S(2)}) %collective-permute-start.71) | collective-permute-done | bytes 4128 | tf_op jit(solution)/shard_map/ppermute | solution.py:156
  94.8 4.2 divide_convert_fusion.3
  99.1 4.6 collective-permute-start.48
  105.0 4.6 collective-permute-start.42
  111.0 10.4 %collective-permute-done.45.refs_0_ = bf16[256,2048]{1,0:T(8,128)(2,1)S(1)} collective-permute-done((bf16[256,2048]{1,0:T(8,128)(2,1)S(1)}, bf16[256,2048]{1,0:T(8,128)(2,1)S(1)}, u32[]{:S(2)}, u32[]{:S(2)}) %collective-permute-start.45) | collective-permute-done | bytes 1048608 | tf_op jit(solution)/shard_map/ppermute | solution.py:146
  122.9 4.3 collective-permute-done.48.refs_1_
  128.4 15.4 %collective-permute-done.39.refs_0_ = bf16[256,2048]{1,0:T(8,128)(2,1)S(1)} collective-permute-done((bf16[256,2048]{1,0:T(8,128)(2,1)S(1)}, bf16[256,2048]{1,0:T(8,128)(2,1)S(1)}, u32[]{:S(2)}, u32[]{:S(2)}) %collective-permute-start.39) | collective-permute-done | bytes 1048608 | tf_op jit(solution)/shard_map/ppermute | solution.py:146
  145.4 4.3 collective-permute-done.42.refs_1_
  150.9 15.4 %collective-permute-done.33.refs_0_ = bf16[256,2048]{1,0:T(8,128)(2,1)S(1)} collective-permute-done((bf16[256,2048]{1,0:T(8,128)(2,1)S(1)}, bf16[256,2048]{1,0:T(8,128)(2,1)S(1)}, u32[]{:S(2)}, u32[]{:S(2)}) %collective-permute-start.33) | collective-permute-done | bytes 1048608 | tf_op jit(solution)/shard_map/ppermute | solution.py:146
  167.8 4.3 collective-permute-done.36.refs_1_
  173.4 15.4 %collective-permute-done.27.refs_0_ = bf16[256,2048]{1,0:T(8,128)(2,1)S(1)} collective-permute-done((bf16[256,2048]{1,0:T(8,128)(2,1)S(1)}, bf16[256,2048]{1,0:T(8,128)(2,1)S(1)}, u32[]{:S(2)}, u32[]{:S(2)}) %collective-permute-start.27) | collective-permute-done | bytes 1048608 | tf_op jit(solution)/shard_map/ppermute | solution.py:146
  190.3 4.3 collective-permute-done.30.refs_1_
  194.6 4.4 collective-permute-start.12
  199.0 12.2 %collective-permute-done.21.refs_0_ = bf16[256,2048]{1,0:T(8,128)(2,1)S(1)} collective-permute-done((bf16[256,2048]{1,0:T(8,128)(2,1)S(1)}, bf16[256,2048]{1,0:T(8,128)(2,1)S(1)}, u32[]{:S(2)}, u32[]{:S(2)}) %collective-permute-start.21) | collective-permute-done | bytes 1048608 | tf_op jit(solution)/shard_map/ppermute | solution.py:146
  212.5 4.5 collective-permute-done.24.refs_1_
  218.3 15.4 %collective-permute-done.15.refs_0_ = bf16[256,2048]{1,0:T(8,128)(2,1)S(1)} collective-permute-done((bf16[256,2048]{1,0:T(8,128)(2,1)S(1)}, bf16[256,2048]{1,0:T(8,128)(2,1)S(1)}, u32[]{:S(2)}, u32[]{:S(2)}) %collective-permute-start.15) | collective-permute-done | bytes 1048608 | tf_op jit(solution)/shard_map/ppermute | solution.py:146
  235.2 4.3 collective-permute-done.18.refs_1_
  240.8 21.2 %collective-permute-done.12.refs_1_ = bf16[256,2048]{1,0:T(8,128)(2,1)S(1)} collective-permute-done((bf16[256,2048]{1,0:T(8,128)(2,1)S(1)}, bf16[256,2048]{1,0:T(8,128)(2,1)S(1)}, u32[]{:S(2)}, u32[]{:S(2)}) %collective-permute-start.12) | collective-permute-done | bytes 1048608 | tf_op jit(solution)/shard_map/ppermute | solution.py:149
  264.0 14.7 %collective-permute-done.3.refs_0_ = bf16[256,2048]{1,0:T(8,128)(2,1)S(1)} collective-permute-done((bf16[256,2048]{1,0:T(8,128)(2,1)S(1)}, bf16[256,2048]{1,0:T(8,128)(2,1)S(1)}, u32[]{:S(2)}, u32[]{:S(2)}) %collective-permute-start.3) | collective-permute-done | bytes 1048608 | tf_op jit(solution)/shard_map/ppermute | solution.py:146
  281.6 19.5 %collective-permute-done.61.refs_0_ = bf16[2048,256]{1,0:T(8,128)(2,1)S(1)} collective-permute-done((bf16[2048,256]{1,0:T(8,128)(2,1)}, bf16[2048,256]{1,0:T(8,128)(2,1)S(1)}, u32[]{:S(2)}, u32[]{:S(2)}) %collective-permute-start.61) | collective-permute-done | bytes 1048608 | tf_op jit(solution)/shard_map/ppermute | solution.py:146
  303.2 20.5 %collective-permute-done.55.refs_0_ = bf16[2048,256]{1,0:T(8,128)(2,1)} collective-permute-done((bf16[2048,256]{1,0:T(8,128)(2,1)}, bf16[2048,256]{1,0:T(8,128)(2,1)}, u32[]{:S(2)}, u32[]{:S(2)}) %collective-permute-start.55) | collective-permute-done | bytes 1048608 | tf_op jit(solution)/shard_map/ppermute | solution.py:146
  325.7 20.3 %collective-permute-done.46.refs_0_ = bf16[256,2048]{1,0:T(8,128)(2,1)S(1)} collective-permute-done((bf16[256,2048]{1,0:T(8,128)(2,1)S(1)}, bf16[256,2048]{1,0:T(8,128)(2,1)S(1)}, u32[]{:S(2)}, u32[]{:S(2)}) %collective-permute-start.46) | collective-permute-done | bytes 1048608 | tf_op jit(solution)/shard_map/ppermute | solution.py:146
  348.1 20.4 %collective-permute-done.40.refs_0_ = bf16[256,2048]{1,0:T(8,128)(2,1)S(1)} collective-permute-done((bf16[256,2048]{1,0:T(8,128)(2,1)S(1)}, bf16[256,2048]{1,0:T(8,128)(2,1)S(1)}, u32[]{:S(2)}, u32[]{:S(2)}) %collective-permute-start.40) | collective-permute-done | bytes 1048608 | tf_op jit(solution)/shard_map/ppermute | solution.py:146
  370.6 20.4 %collective-permute-done.34.refs_0_ = bf16[256,2048]{1,0:T(8,128)(2,1)S(1)} collective-permute-done((bf16[256,2048]{1,0:T(8,128)(2,1)S(1)}, bf16[256,2048]{1,0:T(8,128)(2,1)S(1)}, u32[]{:S(2)}, u32[]{:S(2)}) %collective-permute-start.34) | collective-permute-done | bytes 1048608 | tf_op jit(solution)/shard_map/ppermute | solution.py:146
  393.1 20.4 %collective-permute-done.28.refs_0_ = bf16[256,2048]{1,0:T(8,128)(2,1)S(1)} collective-permute-done((bf16[256,2048]{1,0:T(8,128)(2,1)S(1)}, bf16[256,2048]{1,0:T(8,128)(2,1)S(1)}, u32[]{:S(2)}, u32[]{:S(2)}) %collective-permute-start.28) | collective-permute-done | bytes 1048608 | tf_op jit(solution)/shard_map/ppermute | solution.py:146
  416.5 19.5 %collective-permute-done.22.refs_0_ = bf16[256,2048]{1,0:T(8,128)(2,1)S(1)} collective-permute-done((bf16[256,2048]{1,0:T(8,128)(2,1)S(1)}, bf16[256,2048]{1,0:T(8,128)(2,1)S(1)}, u32[]{:S(2)}, u32[]{:S(2)}) %collective-permute-start.22) | collective-permute-done | bytes 1048608 | tf_op jit(solution)/shard_map/ppermute | solution.py:146
  438.9 19.5 %collective-permute-done.16.refs_0_ = bf16[256,2048]{1,0:T(8,128)(2,1)S(1)} collective-permute-done((bf16[256,2048]{1,0:T(8,128)(2,1)S(1)}, bf16[256,2048]{1,0:T(8,128)(2,1)S(1)}, u32[]{:S(2)}, u32[]{:S(2)}) %collective-permute-start.16) | collective-permute-done | bytes 1048608 | tf_op jit(solution)/shard_map/ppermute | solution.py:146
  461.4 19.6 %collective-permute-done.10.refs_0_ = bf16[256,2048]{1,0:T(8,128)(2,1)} collective-permute-done((bf16[256,2048]{1,0:T(8,128)(2,1)S(1)}, bf16[256,2048]{1,0:T(8,128)(2,1)}, u32[]{:S(2)}, u32[]{:S(2)}) %collective-permute-start.10) | collective-permute-done | bytes 1048608 | tf_op jit(solution)/shard_map/ppermute | solution.py:146
  483.1 20.4 %collective-permute-done.4.refs_0_ = bf16[256,2048]{1,0:T(8,128)(2,1)} collective-permute-done((bf16[256,2048]{1,0:T(8,128)(2,1)S(1)}, bf16[256,2048]{1,0:T(8,128)(2,1)}, u32[]{:S(2)}, u32[]{:S(2)}) %collective-permute-start.4) | collective-permute-done | bytes 1048608 | tf_op jit(solution)/shard_map/ppermute | solution.py:146
  505.5 20.3 %collective-permute-done.62.refs_0_ = bf16[2048,256]{1,0:T(8,128)(2,1)S(1)} collective-permute-done((bf16[2048,256]{1,0:T(8,128)(2,1)S(1)}, bf16[2048,256]{1,0:T(8,128)(2,1)S(1)}, u32[]{:S(2)}, u32[]{:S(2)}) %collective-permute-start.62) | collective-permute-done | bytes 1048608 | tf_op jit(solution)/shard_map/ppermute | solution.py:146
  528.1 20.2 %collective-permute-done.56.refs_0_ = bf16[2048,256]{1,0:T(8,128)(2,1)S(1)} collective-permute-done((bf16[2048,256]{1,0:T(8,128)(2,1)}, bf16[2048,256]{1,0:T(8,128)(2,1)S(1)}, u32[]{:S(2)}, u32[]{:S(2)}) %collective-permute-start.56) | collective-permute-done | bytes 1048608 | tf_op jit(solution)/shard_map/ppermute | solution.py:146
  550.7 20.1 %collective-permute-done.47.refs_0_ = bf16[256,2048]{1,0:T(8,128)(2,1)S(1)} collective-permute-done((bf16[256,2048]{1,0:T(8,128)(2,1)S(1)}, bf16[256,2048]{1,0:T(8,128)(2,1)S(1)}, u32[]{:S(2)}, u32[]{:S(2)}) %collective-permute-start.47) | collective-permute-done | bytes 1048608 | tf_op jit(solution)/shard_map/ppermute | solution.py:146
  572.8 20.4 %collective-permute-done.41.refs_0_ = bf16[256,2048]{1,0:T(8,128)(2,1)S(1)} collective-permute-done((bf16[256,2048]{1,0:T(8,128)(2,1)S(1)}, bf16[256,2048]{1,0:T(8,128)(2,1)S(1)}, u32[]{:S(2)}, u32[]{:S(2)}) %collective-permute-start.41) | collective-permute-done | bytes 1048608 | tf_op jit(solution)/shard_map/ppermute | solution.py:146
  595.3 20.4 %collective-permute-done.35.refs_0_ = bf16[256,2048]{1,0:T(8,128)(2,1)S(1)} collective-permute-done((bf16[256,2048]{1,0:T(8,128)(2,1)S(1)}, bf16[256,2048]{1,0:T(8,128)(2,1)S(1)}, u32[]{:S(2)}, u32[]{:S(2)}) %collective-permute-start.35) | collective-permute-done | bytes 1048608 | tf_op jit(solution)/shard_map/ppermute | solution.py:146
  617.8 20.4 %collective-permute-done.29.refs_0_ = bf16[256,2048]{1,0:T(8,128)(2,1)S(1)} collective-permute-done((bf16[256,2048]{1,0:T(8,128)(2,1)S(1)}, bf16[256,2048]{1,0:T(8,128)(2,1)S(1)}, u32[]{:S(2)}, u32[]{:S(2)}) %collective-permute-start.29) | collective-permute-done | bytes 1048608 | tf_op jit(solution)/shard_map/ppermute | solution.py:146
  641.2 19.5 %collective-permute-done.23.refs_0_ = bf16[256,2048]{1,0:T(8,128)(2,1)S(1)} collective-permute-done((bf16[256,2048]{1,0:T(8,128)(2,1)S(1)}, bf16[256,2048]{1,0:T(8,128)(2,1)S(1)}, u32[]{:S(2)}, u32[]{:S(2)}) %collective-permute-start.23) | collective-permute-done | bytes 1048608 | tf_op jit(solution)/shard_map/ppermute | solution.py:146
  663.6 19.5 %collective-permute-done.17.refs_0_ = bf16[256,2048]{1,0:T(8,128)(2,1)S(1)} collective-permute-done((bf16[256,2048]{1,0:T(8,128)(2,1)S(1)}, bf16[256,2048]{1,0:T(8,128)(2,1)S(1)}, u32[]{:S(2)}, u32[]{:S(2)}) %collective-permute-start.17) | collective-permute-done | bytes 1048608 | tf_op jit(solution)/shard_map/ppermute | solution.py:146
  686.7 2.6 shard_map.171.refs_2_
  689.3 2.6 shard_map.168.refs_2_
  691.9 2.6 shard_map.144.refs_3_
  694.6 2.6 shard_map.145.refs_3_
  697.2 2.6 shard_map.146.refs_3_
  699.8 2.6 shard_map.147.refs_3_
  702.4 2.6 shard_map.148.refs_3_
  705.0 2.6 shard_map.149.refs_3_
  707.6 2.6 shard_map.150.refs_3_
  710.2 2.6 shard_map.151.refs_2_
  715.1 2.2 shard_map.169.refs_2_
  717.3 2.2 shard_map.152.refs_2_
  721.8 2.2 shard_map.154.refs_2_
  724.1 2.2 shard_map.155.refs_2_
  728.6 2.2 shard_map.157.refs_2_
  730.9 2.2 shard_map.158.refs_2_
  735.4 2.2 shard_map.173
  737.6 2.2 shard_map.170
  (280 shorter events, 111.7 us)
Async XLA Ops:
  13.5 32.2 %collective-permute-start = (f32[2048]{0:T(1024)S(1)}, f32[2048]{0:T(1024)S(1)}, u32[]{:S(2)}, u32[]{:S(2)}) collective-permute-start(f32[2048]{0:T(1024)S(1)} %multiply_reduce_fusion), channel_id=1, source_target_pairs={{0,4},{4,8},{8,12},{12,0},{1,5},{5,9},{9,13},{13,1},{2,6},{6,10},{... | collective-permute-start | bytes 24584 | tf_op jit(solution)/shard_map/ppermute | solution.py:88
  16.6 30.4 %collective-permute-start.1 = (f32[2048]{0:T(1024)S(1)}, f32[2048]{0:T(1024)S(1)}, u32[]{:S(2)}, u32[]{:S(2)}) collective-permute-start(f32[2048]{0:T(1024)S(1)} %multiply_reduce_fusion), channel_id=1, source_target_pairs={{0,8},{4,12},{8,0},{12,4},{1,9},{5,13},{9,1},{13,5},{2,10},{6,14},... | collective-permute-start | bytes 24584 | tf_op jit(solution)/shard_map/ppermute | solution.py:88
  32.2 21.2 %collective-permute-start.2 = (f32[2048]{0:T(1024)S(1)}, f32[2048]{0:T(1024)S(1)}, u32[]{:S(2)}, u32[]{:S(2)}) collective-permute-start(f32[2048]{0:T(1024)S(1)} %multiply_reduce_fusion), channel_id=1, source_target_pairs={{0,12},{4,0},{8,4},{12,8},{1,13},{5,1},{9,5},{13,9},{2,14},{6,2},{... | collective-permute-start | bytes 24584 | tf_op jit(solution)/shard_map/ppermute | solution.py:88
  45.8 53.3 %collective-permute-start.60 = (bf16[2048,256]{1,0:T(8,128)(2,1)S(1)}, bf16[2048,256]{1,0:T(8,128)(2,1)}, u32[]{:S(2)}, u32[]{:S(2)}) collective-permute-start(bf16[2048,256]{1,0:T(8,128)(2,1)S(1)} %divide_convert_fusion.refs_2_), channel_id=1, source_target_pairs={{4,0},{8,4},{12,8},{5,1},{9,5},{13,9},{6,2},{10,6},{14,10},{7,3},{... | collective-permute-start | bytes 3145736 | tf_op jit(solution)/shard_map/ppermute | solution.py:146
  47.1 56.6 %collective-permute-start.63 = (bf16[2048,256]{1,0:T(8,128)(2,1)S(1)}, bf16[2048,256]{1,0:T(8,128)(2,1)S(1)}, u32[]{:S(2)}, u32[]{:S(2)}) collective-permute-start(bf16[2048,256]{1,0:T(8,128)(2,1)S(1)} %divide_convert_fusion.refs_2_), channel_id=1, source_target_pairs={{0,4},{4,8},{8,12},{1,5},{5,9},{9,13},{2,6},{6,10},{10,14},{3,7},{... | collective-permute-start | bytes 3145736 | tf_op jit(solution)/shard_map/ppermute | solution.py:149
  53.5 51.5 %collective-permute-start.54 = (bf16[2048,256]{1,0:T(8,128)(2,1)S(1)}, bf16[2048,256]{1,0:T(8,128)(2,1)S(1)}, u32[]{:S(2)}, u32[]{:S(2)}) collective-permute-start(bf16[2048,256]{1,0:T(8,128)(2,1)S(1)} %divide_convert_fusion.1.refs_2_), channel_id=1, source_target_pairs={{4,0},{8,4},{12,8},{5,1},{9,5},{13,9},{6,2},{10,6},{14,10},{7,3},{... | collective-permute-start | bytes 3145736 | tf_op jit(solution)/shard_map/ppermute | solution.py:146
  55.5 38.0 %collective-permute-start.71 = (bf16[2048]{0:T(1024)(128)(2,1)S(1)}, bf16[2048]{0:T(1024)(128)(2,1)S(1)}, u32[]{:S(2)}, u32[]{:S(2)}) collective-permute-start(bf16[2048]{0:T(1024)(128)(2,1)S(1)} %collective-permute-done.70), channel_id=1, source_target_pairs={{4,0},{5,1},{6,2},{7,3},{20,16},{21,17},{22,18},{23,19}} | collective-permute-start | bytes 12296 | tf_op jit(solution)/shard_map/ppermute | solution.py:156
  63.6 46.0 %collective-permute-start.57 = (bf16[2048,256]{1,0:T(8,128)(2,1)S(1)}, bf16[2048,256]{1,0:T(8,128)(2,1)S(1)}, u32[]{:S(2)}, u32[]{:S(2)}) collective-permute-start(bf16[2048,256]{1,0:T(8,128)(2,1)S(1)} %divide_convert_fusion.1.refs_2_), channel_id=1, source_target_pairs={{0,4},{4,8},{8,12},{1,5},{5,9},{9,13},{2,6},{6,10},{10,14},{3,7},{... | collective-permute-start | bytes 3145736 | tf_op jit(solution)/shard_map/ppermute | solution.py:149
  93.5 27.9 %collective-permute-start.45 = (bf16[256,2048]{1,0:T(8,128)(2,1)S(1)}, bf16[256,2048]{1,0:T(8,128)(2,1)S(1)}, u32[]{:S(2)}, u32[]{:S(2)}) collective-permute-start(bf16[256,2048]{1,0:T(8,128)(2,1)S(1)} %get-tuple-element.15.refs_2_), channel_id=1, source_target_pairs={{4,0},{8,4},{12,8},{5,1},{9,5},{13,9},{6,2},{10,6},{14,10},{7,3},{... | collective-permute-start | bytes 3145736 | tf_op jit(solution)/shard_map/ppermute | solution.py:146
  99.1 28.1 %collective-permute-start.48 = (bf16[256,2048]{1,0:T(8,128)(2,1)S(1)}, bf16[256,2048]{1,0:T(8,128)(2,1)S(1)}, u32[]{:S(2)}, u32[]{:S(2)}) collective-permute-start(bf16[256,2048]{1,0:T(8,128)(2,1)S(1)} %get-tuple-element.15.refs_2_), channel_id=1, source_target_pairs={{0,4},{4,8},{8,12},{1,5},{5,9},{9,13},{2,6},{6,10},{10,14},{3,7},{... | collective-permute-start | bytes 3145736 | tf_op jit(solution)/shard_map/ppermute | solution.py:149
  103.7 40.1 %collective-permute-start.39 = (bf16[256,2048]{1,0:T(8,128)(2,1)S(1)}, bf16[256,2048]{1,0:T(8,128)(2,1)S(1)}, u32[]{:S(2)}, u32[]{:S(2)}) collective-permute-start(bf16[256,2048]{1,0:T(8,128)(2,1)S(1)} %get-tuple-element.19.refs_2_), channel_id=1, source_target_pairs={{4,0},{8,4},{12,8},{5,1},{9,5},{13,9},{6,2},{10,6},{14,10},{7,3},{... | collective-permute-start | bytes 3145736 | tf_op jit(solution)/shard_map/ppermute | solution.py:146
  105.0 44.6 %collective-permute-start.42 = (bf16[256,2048]{1,0:T(8,128)(2,1)S(1)}, bf16[256,2048]{1,0:T(8,128)(2,1)S(1)}, u32[]{:S(2)}, u32[]{:S(2)}) collective-permute-start(bf16[256,2048]{1,0:T(8,128)(2,1)S(1)} %get-tuple-element.19.refs_2_), channel_id=1, source_target_pairs={{0,4},{4,8},{8,12},{1,5},{5,9},{9,13},{2,6},{6,10},{10,14},{3,7},{... | collective-permute-start | bytes 3145736 | tf_op jit(solution)/shard_map/ppermute | solution.py:149
  109.7 56.6 %collective-permute-start.33 = (bf16[256,2048]{1,0:T(8,128)(2,1)S(1)}, bf16[256,2048]{1,0:T(8,128)(2,1)S(1)}, u32[]{:S(2)}, u32[]{:S(2)}) collective-permute-start(bf16[256,2048]{1,0:T(8,128)(2,1)S(1)} %get-tuple-element.16.refs_2_), channel_id=1, source_target_pairs={{4,0},{8,4},{12,8},{5,1},{9,5},{13,9},{6,2},{10,6},{14,10},{7,3},{... | collective-permute-start | bytes 3145736 | tf_op jit(solution)/shard_map/ppermute | solution.py:146
  121.4 50.7 %collective-permute-start.36 = (bf16[256,2048]{1,0:T(8,128)(2,1)S(1)}, bf16[256,2048]{1,0:T(8,128)(2,1)S(1)}, u32[]{:S(2)}, u32[]{:S(2)}) collective-permute-start(bf16[256,2048]{1,0:T(8,128)(2,1)S(1)} %get-tuple-element.16.refs_2_), channel_id=1, source_target_pairs={{0,4},{4,8},{8,12},{1,5},{5,9},{9,13},{2,6},{6,10},{10,14},{3,7},{... | collective-permute-start | bytes 3145736 | tf_op jit(solution)/shard_map/ppermute | solution.py:149
  127.1 61.6 %collective-permute-start.27 = (bf16[256,2048]{1,0:T(8,128)(2,1)S(1)}, bf16[256,2048]{1,0:T(8,128)(2,1)S(1)}, u32[]{:S(2)}, u32[]{:S(2)}) collective-permute-start(bf16[256,2048]{1,0:T(8,128)(2,1)S(1)} %get-tuple-element.17.refs_2_), channel_id=1, source_target_pairs={{4,0},{8,4},{12,8},{5,1},{9,5},{13,9},{6,2},{10,6},{14,10},{7,3},{... | collective-permute-start | bytes 3145736 | tf_op jit(solution)/shard_map/ppermute | solution.py:146
  143.8 50.7 %collective-permute-start.30 = (bf16[256,2048]{1,0:T(8,128)(2,1)S(1)}, bf16[256,2048]{1,0:T(8,128)(2,1)S(1)}, u32[]{:S(2)}, u32[]{:S(2)}) collective-permute-start(bf16[256,2048]{1,0:T(8,128)(2,1)S(1)} %get-tuple-element.17.refs_2_), channel_id=1, source_target_pairs={{0,4},{4,8},{8,12},{1,5},{5,9},{9,13},{2,6},{6,10},{10,14},{3,7},{... | collective-permute-start | bytes 3145736 | tf_op jit(solution)/shard_map/ppermute | solution.py:149
  149.6 61.6 %collective-permute-start.21 = (bf16[256,2048]{1,0:T(8,128)(2,1)S(1)}, bf16[256,2048]{1,0:T(8,128)(2,1)S(1)}, u32[]{:S(2)}, u32[]{:S(2)}) collective-permute-start(bf16[256,2048]{1,0:T(8,128)(2,1)S(1)} %get-tuple-element.18.refs_2_), channel_id=1, source_target_pairs={{4,0},{8,4},{12,8},{5,1},{9,5},{13,9},{6,2},{10,6},{14,10},{7,3},{... | collective-permute-start | bytes 3145736 | tf_op jit(solution)/shard_map/ppermute | solution.py:146
  166.3 50.7 %collective-permute-start.24 = (bf16[256,2048]{1,0:T(8,128)(2,1)S(1)}, bf16[256,2048]{1,0:T(8,128)(2,1)S(1)}, u32[]{:S(2)}, u32[]{:S(2)}) collective-permute-start(bf16[256,2048]{1,0:T(8,128)(2,1)S(1)} %get-tuple-element.18.refs_2_), channel_id=1, source_target_pairs={{0,4},{4,8},{8,12},{1,5},{5,9},{9,13},{2,6},{6,10},{10,14},{3,7},{... | collective-permute-start | bytes 3145736 | tf_op jit(solution)/shard_map/ppermute | solution.py:149
  172.1 61.6 %collective-permute-start.15 = (bf16[256,2048]{1,0:T(8,128)(2,1)S(1)}, bf16[256,2048]{1,0:T(8,128)(2,1)S(1)}, u32[]{:S(2)}, u32[]{:S(2)}) collective-permute-start(bf16[256,2048]{1,0:T(8,128)(2,1)S(1)} %get-tuple-element.20.refs_2_), channel_id=1, source_target_pairs={{4,0},{8,4},{12,8},{5,1},{9,5},{13,9},{6,2},{10,6},{14,10},{7,3},{... | collective-permute-start | bytes 3145736 | tf_op jit(solution)/shard_map/ppermute | solution.py:146
  188.8 50.7 %collective-permute-start.18 = (bf16[256,2048]{1,0:T(8,128)(2,1)S(1)}, bf16[256,2048]{1,0:T(8,128)(2,1)S(1)}, u32[]{:S(2)}, u32[]{:S(2)}) collective-permute-start(bf16[256,2048]{1,0:T(8,128)(2,1)S(1)} %get-tuple-element.20.refs_2_), channel_id=1, source_target_pairs={{0,4},{4,8},{8,12},{1,5},{5,9},{9,13},{2,6},{6,10},{10,14},{3,7},{... | collective-permute-start | bytes 3145736 | tf_op jit(solution)/shard_map/ppermute | solution.py:149
  194.6 67.4 %collective-permute-start.12 = (bf16[256,2048]{1,0:T(8,128)(2,1)S(1)}, bf16[256,2048]{1,0:T(8,128)(2,1)S(1)}, u32[]{:S(2)}, u32[]{:S(2)}) collective-permute-start(bf16[256,2048]{1,0:T(8,128)(2,1)S(1)} %get-tuple-element.21.refs_2_), channel_id=1, source_target_pairs={{0,4},{4,8},{8,12},{1,5},{5,9},{9,13},{2,6},{6,10},{10,14},{3,7},{... | collective-permute-start | bytes 3145736 | tf_op jit(solution)/shard_map/ppermute | solution.py:149
  211.2 51.4 %collective-permute-start.9 = (bf16[256,2048]{1,0:T(8,128)(2,1)S(1)}, bf16[256,2048]{1,0:T(8,128)(2,1)S(1)}, u32[]{:S(2)}, u32[]{:S(2)}) collective-permute-start(bf16[256,2048]{1,0:T(8,128)(2,1)S(1)} %get-tuple-element.21.refs_2_), channel_id=1, source_target_pairs={{4,0},{8,4},{12,8},{5,1},{9,5},{13,9},{6,2},{10,6},{14,10},{7,3},{... | collective-permute-start | bytes 3145736 | tf_op jit(solution)/shard_map/ppermute | solution.py:146
  217.0 61.6 %collective-permute-start.3 = (bf16[256,2048]{1,0:T(8,128)(2,1)S(1)}, bf16[256,2048]{1,0:T(8,128)(2,1)S(1)}, u32[]{:S(2)}, u32[]{:S(2)}) collective-permute-start(bf16[256,2048]{1,0:T(8,128)(2,1)S(1)} %get-tuple-element.22.refs_2_), channel_id=1, source_target_pairs={{4,0},{8,4},{12,8},{5,1},{9,5},{13,9},{6,2},{10,6},{14,10},{7,3},{... | collective-permute-start | bytes 3145736 | tf_op jit(solution)/shard_map/ppermute | solution.py:146
  233.7 46.6 %collective-permute-start.6 = (bf16[256,2048]{1,0:T(8,128)(2,1)S(1)}, bf16[256,2048]{1,0:T(8,128)(2,1)S(1)}, u32[]{:S(2)}, u32[]{:S(2)}) collective-permute-start(bf16[256,2048]{1,0:T(8,128)(2,1)S(1)} %get-tuple-element.22.refs_2_), channel_id=1, source_target_pairs={{0,4},{4,8},{8,12},{1,5},{5,9},{9,13},{2,6},{6,10},{10,14},{3,7},{... | collective-permute-start | bytes 3145736 | tf_op jit(solution)/shard_map/ppermute | solution.py:149
  239.5 61.6 %collective-permute-start.61 = (bf16[2048,256]{1,0:T(8,128)(2,1)}, bf16[2048,256]{1,0:T(8,128)(2,1)S(1)}, u32[]{:S(2)}, u32[]{:S(2)}) collective-permute-start(bf16[2048,256]{1,0:T(8,128)(2,1)} %collective-permute-done.60.refs_0_), channel_id=1, source_target_pairs={{4,0},{8,4},{5,1},{9,5},{6,2},{10,6},{7,3},{11,7},{20,16},{24,20},... | collective-permute-start | bytes 3145736 | tf_op jit(solution)/shard_map/ppermute | solution.py:146
  262.0 39.9 %collective-permute-start.64 = (bf16[2048,256]{1,0:T(8,128)(2,1)}, bf16[2048,256]{1,0:T(8,128)(2,1)S(1)}, u32[]{:S(2)}, u32[]{:S(2)}) collective-permute-start(bf16[2048,256]{1,0:T(8,128)(2,1)} %copy-done.58), channel_id=1, source_target_pairs={{4,8},{8,12},{5,9},{9,13},{6,10},{10,14},{7,11},{11,15},{20,24},{2... | collective-permute-start | bytes 3145736 | tf_op jit(solution)/shard_map/ppermute | solution.py:149
  262.7 61.0 %collective-permute-start.55 = (bf16[2048,256]{1,0:T(8,128)(2,1)}, bf16[2048,256]{1,0:T(8,128)(2,1)}, u32[]{:S(2)}, u32[]{:S(2)}) collective-permute-start(bf16[2048,256]{1,0:T(8,128)(2,1)} %copy-done.59), channel_id=1, source_target_pairs={{4,0},{8,4},{5,1},{9,5},{6,2},{10,6},{7,3},{11,7},{20,16},{24,20},... | collective-permute-start | bytes 3145736 | tf_op jit(solution)/shard_map/ppermute | solution.py:146
  278.7 45.8 %collective-permute-start.58 = (bf16[2048,256]{1,0:T(8,128)(2,1)}, bf16[2048,256]{1,0:T(8,128)(2,1)}, u32[]{:S(2)}, u32[]{:S(2)}) collective-permute-start(bf16[2048,256]{1,0:T(8,128)(2,1)} %copy-done.60), channel_id=1, source_target_pairs={{4,8},{8,12},{5,9},{9,13},{6,10},{10,14},{7,11},{11,15},{20,24},{2... | collective-permute-start | bytes 3145736 | tf_op jit(solution)/shard_map/ppermute | solution.py:149
  280.3 65.8 %collective-permute-start.46 = (bf16[256,2048]{1,0:T(8,128)(2,1)S(1)}, bf16[256,2048]{1,0:T(8,128)(2,1)S(1)}, u32[]{:S(2)}, u32[]{:S(2)}) collective-permute-start(bf16[256,2048]{1,0:T(8,128)(2,1)S(1)} %collective-permute-done.45.refs_0_), channel_id=1, source_target_pairs={{4,0},{8,4},{5,1},{9,5},{6,2},{10,6},{7,3},{11,7},{20,16},{24,20},... | collective-permute-start | bytes 3145736 | tf_op jit(solution)/shard_map/ppermute | solution.py:146
  301.1 45.7 %collective-permute-start.49 = (bf16[256,2048]{1,0:T(8,128)(2,1)S(1)}, bf16[256,2048]{1,0:T(8,128)(2,1)S(1)}, u32[]{:S(2)}, u32[]{:S(2)}) collective-permute-start(bf16[256,2048]{1,0:T(8,128)(2,1)S(1)} %collective-permute-done.48.refs_1_), channel_id=1, source_target_pairs={{4,8},{8,12},{5,9},{9,13},{6,10},{10,14},{7,11},{11,15},{20,24},{2... | collective-permute-start | bytes 3145736 | tf_op jit(solution)/shard_map/ppermute | solution.py:149
  301.9 66.7 %collective-permute-start.40 = (bf16[256,2048]{1,0:T(8,128)(2,1)S(1)}, bf16[256,2048]{1,0:T(8,128)(2,1)S(1)}, u32[]{:S(2)}, u32[]{:S(2)}) collective-permute-start(bf16[256,2048]{1,0:T(8,128)(2,1)S(1)} %collective-permute-done.39.refs_0_), channel_id=1, source_target_pairs={{4,0},{8,4},{5,1},{9,5},{6,2},{10,6},{7,3},{11,7},{20,16},{24,20},... | collective-permute-start | bytes 3145736 | tf_op jit(solution)/shard_map/ppermute | solution.py:146
  323.7 45.6 %collective-permute-start.43 = (bf16[256,2048]{1,0:T(8,128)(2,1)S(1)}, bf16[256,2048]{1,0:T(8,128)(2,1)S(1)}, u32[]{:S(2)}, u32[]{:S(2)}) collective-permute-start(bf16[256,2048]{1,0:T(8,128)(2,1)S(1)} %collective-permute-done.42.refs_1_), channel_id=1, source_target_pairs={{4,8},{8,12},{5,9},{9,13},{6,10},{10,14},{7,11},{11,15},{20,24},{2... | collective-permute-start | bytes 3145736 | tf_op jit(solution)/shard_map/ppermute | solution.py:149
  324.4 66.6 %collective-permute-start.34 = (bf16[256,2048]{1,0:T(8,128)(2,1)S(1)}, bf16[256,2048]{1,0:T(8,128)(2,1)S(1)}, u32[]{:S(2)}, u32[]{:S(2)}) collective-permute-start(bf16[256,2048]{1,0:T(8,128)(2,1)S(1)} %collective-permute-done.33.refs_0_), channel_id=1, source_target_pairs={{4,0},{8,4},{5,1},{9,5},{6,2},{10,6},{7,3},{11,7},{20,16},{24,20},... | collective-permute-start | bytes 3145736 | tf_op jit(solution)/shard_map/ppermute | solution.py:146
  346.1 45.7 %collective-permute-start.37 = (bf16[256,2048]{1,0:T(8,128)(2,1)S(1)}, bf16[256,2048]{1,0:T(8,128)(2,1)S(1)}, u32[]{:S(2)}, u32[]{:S(2)}) collective-permute-start(bf16[256,2048]{1,0:T(8,128)(2,1)S(1)} %collective-permute-done.36.refs_1_), channel_id=1, source_target_pairs={{4,8},{8,12},{5,9},{9,13},{6,10},{10,14},{7,11},{11,15},{20,24},{2... | collective-permute-start | bytes 3145736 | tf_op jit(solution)/shard_map/ppermute | solution.py:149
  346.8 66.7 %collective-permute-start.28 = (bf16[256,2048]{1,0:T(8,128)(2,1)S(1)}, bf16[256,2048]{1,0:T(8,128)(2,1)S(1)}, u32[]{:S(2)}, u32[]{:S(2)}) collective-permute-start(bf16[256,2048]{1,0:T(8,128)(2,1)S(1)} %collective-permute-done.27.refs_0_), channel_id=1, source_target_pairs={{4,0},{8,4},{5,1},{9,5},{6,2},{10,6},{7,3},{11,7},{20,16},{24,20},... | collective-permute-start | bytes 3145736 | tf_op jit(solution)/shard_map/ppermute | solution.py:146
  368.5 46.6 %collective-permute-start.31 = (bf16[256,2048]{1,0:T(8,128)(2,1)S(1)}, bf16[256,2048]{1,0:T(8,128)(2,1)S(1)}, u32[]{:S(2)}, u32[]{:S(2)}) collective-permute-start(bf16[256,2048]{1,0:T(8,128)(2,1)S(1)} %collective-permute-done.30.refs_1_), channel_id=1, source_target_pairs={{4,8},{8,12},{5,9},{9,13},{6,10},{10,14},{7,11},{11,15},{20,24},{2... | collective-permute-start | bytes 3145736 | tf_op jit(solution)/shard_map/ppermute | solution.py:149
  369.3 66.7 %collective-permute-start.22 = (bf16[256,2048]{1,0:T(8,128)(2,1)S(1)}, bf16[256,2048]{1,0:T(8,128)(2,1)S(1)}, u32[]{:S(2)}, u32[]{:S(2)}) collective-permute-start(bf16[256,2048]{1,0:T(8,128)(2,1)S(1)} %collective-permute-done.21.refs_0_), channel_id=1, source_target_pairs={{4,0},{8,4},{5,1},{9,5},{6,2},{10,6},{7,3},{11,7},{20,16},{24,20},... | collective-permute-start | bytes 3145736 | tf_op jit(solution)/shard_map/ppermute | solution.py:146
  391.0 46.6 %collective-permute-start.25 = (bf16[256,2048]{1,0:T(8,128)(2,1)S(1)}, bf16[256,2048]{1,0:T(8,128)(2,1)S(1)}, u32[]{:S(2)}, u32[]{:S(2)}) collective-permute-start(bf16[256,2048]{1,0:T(8,128)(2,1)S(1)} %collective-permute-done.24.refs_1_), channel_id=1, source_target_pairs={{4,8},{8,12},{5,9},{9,13},{6,10},{10,14},{7,11},{11,15},{20,24},{2... | collective-permute-start | bytes 3145736 | tf_op jit(solution)/shard_map/ppermute | solution.py:149
  391.8 66.7 %collective-permute-start.16 = (bf16[256,2048]{1,0:T(8,128)(2,1)S(1)}, bf16[256,2048]{1,0:T(8,128)(2,1)S(1)}, u32[]{:S(2)}, u32[]{:S(2)}) collective-permute-start(bf16[256,2048]{1,0:T(8,128)(2,1)S(1)} %collective-permute-done.15.refs_0_), channel_id=1, source_target_pairs={{4,0},{8,4},{5,1},{9,5},{6,2},{10,6},{7,3},{11,7},{20,16},{24,20},... | collective-permute-start | bytes 3145736 | tf_op jit(solution)/shard_map/ppermute | solution.py:146
  413.5 46.6 %collective-permute-start.19 = (bf16[256,2048]{1,0:T(8,128)(2,1)S(1)}, bf16[256,2048]{1,0:T(8,128)(2,1)}, u32[]{:S(2)}, u32[]{:S(2)}) collective-permute-start(bf16[256,2048]{1,0:T(8,128)(2,1)S(1)} %collective-permute-done.18.refs_1_), channel_id=1, source_target_pairs={{4,8},{8,12},{5,9},{9,13},{6,10},{10,14},{7,11},{11,15},{20,24},{2... | collective-permute-start | bytes 3145736 | tf_op jit(solution)/shard_map/ppermute | solution.py:149
  415.2 65.8 %collective-permute-start.10 = (bf16[256,2048]{1,0:T(8,128)(2,1)S(1)}, bf16[256,2048]{1,0:T(8,128)(2,1)}, u32[]{:S(2)}, u32[]{:S(2)}) collective-permute-start(bf16[256,2048]{1,0:T(8,128)(2,1)S(1)} %collective-permute-done.9.refs_0_), channel_id=1, source_target_pairs={{4,0},{8,4},{5,1},{9,5},{6,2},{10,6},{7,3},{11,7},{20,16},{24,20},... | collective-permute-start | bytes 3145736 | tf_op jit(solution)/shard_map/ppermute | solution.py:146
  436.0 45.8 %collective-permute-start.13 = (bf16[256,2048]{1,0:T(8,128)(2,1)S(1)}, bf16[256,2048]{1,0:T(8,128)(2,1)}, u32[]{:S(2)}, u32[]{:S(2)}) collective-permute-start(bf16[256,2048]{1,0:T(8,128)(2,1)S(1)} %collective-permute-done.12.refs_1_), channel_id=1, source_target_pairs={{4,8},{8,12},{5,9},{9,13},{6,10},{10,14},{7,11},{11,15},{20,24},{2... | collective-permute-start | bytes 3145736 | tf_op jit(solution)/shard_map/ppermute | solution.py:149
  437.6 65.8 %collective-permute-start.4 = (bf16[256,2048]{1,0:T(8,128)(2,1)S(1)}, bf16[256,2048]{1,0:T(8,128)(2,1)}, u32[]{:S(2)}, u32[]{:S(2)}) collective-permute-start(bf16[256,2048]{1,0:T(8,128)(2,1)S(1)} %collective-permute-done.3.refs_0_), channel_id=1, source_target_pairs={{4,0},{8,4},{5,1},{9,5},{6,2},{10,6},{7,3},{11,7},{20,16},{24,20},... | collective-permute-start | bytes 3145736 | tf_op jit(solution)/shard_map/ppermute | solution.py:146
  458.4 45.8 %collective-permute-start.7 = (bf16[256,2048]{1,0:T(8,128)(2,1)S(1)}, bf16[256,2048]{1,0:T(8,128)(2,1)}, u32[]{:S(2)}, u32[]{:S(2)}) collective-permute-start(bf16[256,2048]{1,0:T(8,128)(2,1)S(1)} %collective-permute-done.6.refs_1_), channel_id=1, source_target_pairs={{4,8},{8,12},{5,9},{9,13},{6,10},{10,14},{7,11},{11,15},{20,24},{2... | collective-permute-start | bytes 3145736 | tf_op jit(solution)/shard_map/ppermute | solution.py:149
  460.1 65.7 %collective-permute-start.62 = (bf16[2048,256]{1,0:T(8,128)(2,1)S(1)}, bf16[2048,256]{1,0:T(8,128)(2,1)S(1)}, u32[]{:S(2)}, u32[]{:S(2)}) collective-permute-start(bf16[2048,256]{1,0:T(8,128)(2,1)S(1)} %collective-permute-done.61.refs_0_), channel_id=1, source_target_pairs={{4,0},{5,1},{6,2},{7,3},{20,16},{21,17},{22,18},{23,19}} | collective-permute-start | bytes 3145736 | tf_op jit(solution)/shard_map/ppermute | solution.py:146
  481.0 45.8 %collective-permute-start.65 = (bf16[2048,256]{1,0:T(8,128)(2,1)S(1)}, bf16[2048,256]{1,0:T(8,128)(2,1)S(1)}, u32[]{:S(2)}, u32[]{:S(2)}) collective-permute-start(bf16[2048,256]{1,0:T(8,128)(2,1)S(1)} %collective-permute-done.64.refs_1_), channel_id=1, source_target_pairs={{8,12},{9,13},{10,14},{11,15},{24,28},{25,29},{26,30},{27,31}} | collective-permute-start | bytes 3145736 | tf_op jit(solution)/shard_map/ppermute | solution.py:149
  481.7 66.6 %collective-permute-start.56 = (bf16[2048,256]{1,0:T(8,128)(2,1)}, bf16[2048,256]{1,0:T(8,128)(2,1)S(1)}, u32[]{:S(2)}, u32[]{:S(2)}) collective-permute-start(bf16[2048,256]{1,0:T(8,128)(2,1)} %collective-permute-done.55.refs_0_), channel_id=1, source_target_pairs={{4,0},{5,1},{6,2},{7,3},{20,16},{21,17},{22,18},{23,19}} | collective-permute-start | bytes 3145736 | tf_op jit(solution)/shard_map/ppermute | solution.py:146
  503.5 45.9 %collective-permute-start.59 = (bf16[2048,256]{1,0:T(8,128)(2,1)}, bf16[2048,256]{1,0:T(8,128)(2,1)S(1)}, u32[]{:S(2)}, u32[]{:S(2)}) collective-permute-start(bf16[2048,256]{1,0:T(8,128)(2,1)} %collective-permute-done.58.refs_1_), channel_id=1, source_target_pairs={{8,12},{9,13},{10,14},{11,15},{24,28},{25,29},{26,30},{27,31}} | collective-permute-start | bytes 3145736 | tf_op jit(solution)/shard_map/ppermute | solution.py:149
  504.2 66.6 %collective-permute-start.47 = (bf16[256,2048]{1,0:T(8,128)(2,1)S(1)}, bf16[256,2048]{1,0:T(8,128)(2,1)S(1)}, u32[]{:S(2)}, u32[]{:S(2)}) collective-permute-start(bf16[256,2048]{1,0:T(8,128)(2,1)S(1)} %collective-permute-done.46.refs_0_), channel_id=1, source_target_pairs={{4,0},{5,1},{6,2},{7,3},{20,16},{21,17},{22,18},{23,19}} | collective-permute-start | bytes 3145736 | tf_op jit(solution)/shard_map/ppermute | solution.py:146
  525.8 45.7 %collective-permute-start.50 = (bf16[256,2048]{1,0:T(8,128)(2,1)S(1)}, bf16[256,2048]{1,0:T(8,128)(2,1)S(1)}, u32[]{:S(2)}, u32[]{:S(2)}) collective-permute-start(bf16[256,2048]{1,0:T(8,128)(2,1)S(1)} %collective-permute-done.49.refs_1_), channel_id=1, source_target_pairs={{8,12},{9,13},{10,14},{11,15},{24,28},{25,29},{26,30},{27,31}} | collective-permute-start | bytes 3145736 | tf_op jit(solution)/shard_map/ppermute | solution.py:149
  526.8 66.5 %collective-permute-start.41 = (bf16[256,2048]{1,0:T(8,128)(2,1)S(1)}, bf16[256,2048]{1,0:T(8,128)(2,1)S(1)}, u32[]{:S(2)}, u32[]{:S(2)}) collective-permute-start(bf16[256,2048]{1,0:T(8,128)(2,1)S(1)} %collective-permute-done.40.refs_0_), channel_id=1, source_target_pairs={{4,0},{5,1},{6,2},{7,3},{20,16},{21,17},{22,18},{23,19}} | collective-permute-start | bytes 3145736 | tf_op jit(solution)/shard_map/ppermute | solution.py:146
  548.3 45.7 %collective-permute-start.44 = (bf16[256,2048]{1,0:T(8,128)(2,1)S(1)}, bf16[256,2048]{1,0:T(8,128)(2,1)S(1)}, u32[]{:S(2)}, u32[]{:S(2)}) collective-permute-start(bf16[256,2048]{1,0:T(8,128)(2,1)S(1)} %collective-permute-done.43.refs_1_), channel_id=1, source_target_pairs={{8,12},{9,13},{10,14},{11,15},{24,28},{25,29},{26,30},{27,31}} | collective-permute-start | bytes 3145736 | tf_op jit(solution)/shard_map/ppermute | solution.py:149
  549.4 66.4 %collective-permute-start.35 = (bf16[256,2048]{1,0:T(8,128)(2,1)S(1)}, bf16[256,2048]{1,0:T(8,128)(2,1)S(1)}, u32[]{:S(2)}, u32[]{:S(2)}) collective-permute-start(bf16[256,2048]{1,0:T(8,128)(2,1)S(1)} %collective-permute-done.34.refs_0_), channel_id=1, source_target_pairs={{4,0},{5,1},{6,2},{7,3},{20,16},{21,17},{22,18},{23,19}} | collective-permute-start | bytes 3145736 | tf_op jit(solution)/shard_map/ppermute | solution.py:146
  570.8 45.7 %collective-permute-start.38 = (bf16[256,2048]{1,0:T(8,128)(2,1)S(1)}, bf16[256,2048]{1,0:T(8,128)(2,1)S(1)}, u32[]{:S(2)}, u32[]{:S(2)}) collective-permute-start(bf16[256,2048]{1,0:T(8,128)(2,1)S(1)} %collective-permute-done.37.refs_1_), channel_id=1, source_target_pairs={{8,12},{9,13},{10,14},{11,15},{24,28},{25,29},{26,30},{27,31}} | collective-permute-start | bytes 3145736 | tf_op jit(solution)/shard_map/ppermute | solution.py:149
  571.5 66.7 %collective-permute-start.29 = (bf16[256,2048]{1,0:T(8,128)(2,1)S(1)}, bf16[256,2048]{1,0:T(8,128)(2,1)S(1)}, u32[]{:S(2)}, u32[]{:S(2)}) collective-permute-start(bf16[256,2048]{1,0:T(8,128)(2,1)S(1)} %collective-permute-done.28.refs_0_), channel_id=1, source_target_pairs={{4,0},{5,1},{6,2},{7,3},{20,16},{21,17},{22,18},{23,19}} | collective-permute-start | bytes 3145736 | tf_op jit(solution)/shard_map/ppermute | solution.py:146
  593.3 46.7 %collective-permute-start.32 = (bf16[256,2048]{1,0:T(8,128)(2,1)S(1)}, bf16[256,2048]{1,0:T(8,128)(2,1)S(1)}, u32[]{:S(2)}, u32[]{:S(2)}) collective-permute-start(bf16[256,2048]{1,0:T(8,128)(2,1)S(1)} %collective-permute-done.31.refs_1_), channel_id=1, source_target_pairs={{8,12},{9,13},{10,14},{11,15},{24,28},{25,29},{26,30},{27,31}} | collective-permute-start | bytes 3145736 | tf_op jit(solution)/shard_map/ppermute | solution.py:149
  594.0 66.6 %collective-permute-start.23 = (bf16[256,2048]{1,0:T(8,128)(2,1)S(1)}, bf16[256,2048]{1,0:T(8,128)(2,1)S(1)}, u32[]{:S(2)}, u32[]{:S(2)}) collective-permute-start(bf16[256,2048]{1,0:T(8,128)(2,1)S(1)} %collective-permute-done.22.refs_0_), channel_id=1, source_target_pairs={{4,0},{5,1},{6,2},{7,3},{20,16},{21,17},{22,18},{23,19}} | collective-permute-start | bytes 3145736 | tf_op jit(solution)/shard_map/ppermute | solution.py:146
  615.7 46.6 %collective-permute-start.26 = (bf16[256,2048]{1,0:T(8,128)(2,1)S(1)}, bf16[256,2048]{1,0:T(8,128)(2,1)S(1)}, u32[]{:S(2)}, u32[]{:S(2)}) collective-permute-start(bf16[256,2048]{1,0:T(8,128)(2,1)S(1)} %collective-permute-done.25.refs_1_), channel_id=1, source_target_pairs={{8,12},{9,13},{10,14},{11,15},{24,28},{25,29},{26,30},{27,31}} | collective-permute-start | bytes 3145736 | tf_op jit(solution)/shard_map/ppermute | solution.py:149
  616.5 66.7 %collective-permute-start.17 = (bf16[256,2048]{1,0:T(8,128)(2,1)S(1)}, bf16[256,2048]{1,0:T(8,128)(2,1)S(1)}, u32[]{:S(2)}, u32[]{:S(2)}) collective-permute-start(bf16[256,2048]{1,0:T(8,128)(2,1)S(1)} %collective-permute-done.16.refs_0_), channel_id=1, source_target_pairs={{4,0},{5,1},{6,2},{7,3},{20,16},{21,17},{22,18},{23,19}} | collective-permute-start | bytes 3145736 | tf_op jit(solution)/shard_map/ppermute | solution.py:146
  638.2 112.9 %collective-permute-start.20 = (bf16[256,2048]{1,0:T(8,128)(2,1)}, bf16[256,2048]{1,0:T(8,128)(2,1)}, u32[]{:S(2)}, u32[]{:S(2)}) collective-permute-start(bf16[256,2048]{1,0:T(8,128)(2,1)} %collective-permute-done.19.refs_1_), channel_id=1, source_target_pairs={{8,12},{9,13},{10,14},{11,15},{24,28},{25,29},{26,30},{27,31}} | collective-permute-start | bytes 3145736 | tf_op jit(solution)/shard_map/ppermute | solution.py:149
  639.9 113.5 %collective-permute-start.11 = (bf16[256,2048]{1,0:T(8,128)(2,1)}, bf16[256,2048]{1,0:T(8,128)(2,1)}, u32[]{:S(2)}, u32[]{:S(2)}) collective-permute-start(bf16[256,2048]{1,0:T(8,128)(2,1)} %collective-permute-done.10.refs_0_), channel_id=1, source_target_pairs={{4,0},{5,1},{6,2},{7,3},{20,16},{21,17},{22,18},{23,19}} | collective-permute-start | bytes 3145736 | tf_op jit(solution)/shard_map/ppermute | solution.py:146
  660.7 92.7 %collective-permute-start.14 = (bf16[256,2048]{1,0:T(8,128)(2,1)}, bf16[256,2048]{1,0:T(8,128)(2,1)}, u32[]{:S(2)}, u32[]{:S(2)}) collective-permute-start(bf16[256,2048]{1,0:T(8,128)(2,1)} %collective-permute-done.13.refs_1_), channel_id=1, source_target_pairs={{8,12},{9,13},{10,14},{11,15},{24,28},{25,29},{26,30},{27,31}} | collective-permute-start | bytes 3145736 | tf_op jit(solution)/shard_map/ppermute | solution.py:149
  662.3 93.3 %collective-permute-start.5 = (bf16[256,2048]{1,0:T(8,128)(2,1)}, bf16[256,2048]{1,0:T(8,128)(2,1)}, u32[]{:S(2)}, u32[]{:S(2)}) collective-permute-start(bf16[256,2048]{1,0:T(8,128)(2,1)} %collective-permute-done.4.refs_0_), channel_id=1, source_target_pairs={{4,0},{5,1},{6,2},{7,3},{20,16},{21,17},{22,18},{23,19}} | collective-permute-start | bytes 3145736 | tf_op jit(solution)/shard_map/ppermute | solution.py:146
  684.2 71.5 %collective-permute-start.8 = (bf16[256,2048]{1,0:T(8,128)(2,1)}, bf16[256,2048]{1,0:T(8,128)(2,1)}, u32[]{:S(2)}, u32[]{:S(2)}) collective-permute-start(bf16[256,2048]{1,0:T(8,128)(2,1)} %collective-permute-done.7.refs_1_), channel_id=1, source_target_pairs={{8,12},{9,13},{10,14},{11,15},{24,28},{25,29},{26,30},{27,31}} | collective-permute-start | bytes 3145736 | tf_op jit(solution)/shard_map/ppermute | solution.py:149
  (79 other events, 8945.3 us)
